TPU v7x, 256 devices: a whole 4x4x8 slice. The times are simulated.
256 devices in a mesh: dp: 16 (over x, z_lo), owner: 16 (over z_hi, y, core).
Axes of the slice: x: 4, y: 4, z: 8 (z_hi: 2, z_lo: 4; z = z_hi * 4 + z_lo), core: 2. Of those that a mesh axis runs over, the one named last changes fastest.
Arguments:
- layer_input: bfloat16 [4096, 8192], P('dp', 'owner'), may hold values from -6 to 6
- output_grads: bfloat16 [4096, 10240], P('dp', 'owner'), may hold values from -6 to 6
- projection: bfloat16 [8192, 10240], P('owner', 'dp'), may hold values from -0.0625 to 0.0625
Outputs:
- grad_input: bfloat16 [4096, 8192], P('dp', 'owner')
- update_query: bfloat16 [8192, 8192], P('owner', 'dp')
- update_kv: bfloat16 [8192, 2048], P('owner', 'dp')
All inputs are finite; a program needn't handle non-finite values.
Results may differ from a plain program's by a relative error of at most 0.023.
Values may be sent and summed in bfloat16 or wider, within the bound.
A program may use at most 128 MiB of HBM per device.

v0:
```python
import math

import jax
import jax.numpy as jnp
from jax import lax
from jax.sharding import Mesh
from jax.sharding import PartitionSpec as P

BLOCK = 512
QW = 8192
DP = ("dp_0", "dp_1")


def gather_axes(shard, axes, dim):
    whole = shard
    for number in range(len(axes) - 1, -1, -1):
        whole = lax.all_gather(whole, axes[number], axis=dim, tiled=True)
    return whole


def split_up(shard, dim, devices):
    before, after = (shard.shape[:dim], shard.shape[dim + 1 :])
    return jnp.moveaxis(shard.reshape(*before, devices, -1, *after), dim, 0)


def sum_at_owner(shard, axis, dim):
    devices = lax.axis_size(axis)
    blocks = lax.all_to_all(split_up(shard, dim, devices), axis, 0, 0, tiled=True)
    return jnp.sum(blocks.astype(jnp.float32), axis=0)


def left_stat(blocks):
    return jnp.einsum("...ij,...kj->...ik", blocks, blocks, preferred_element_type=jnp.float32)


def right_stat(blocks):
    return jnp.einsum("...ji,...jk->...ik", blocks, blocks, preferred_element_type=jnp.float32)


def inverse_root(statistic):
    width = statistic.shape[-1]
    scale = math.sqrt(width) * jnp.sqrt(
        jnp.mean(statistic * statistic, axis=(-2, -1), keepdims=True) + 1e-06
    )
    normed = statistic / scale
    identity = jnp.eye(width, dtype=jnp.float32)
    return scale ** (-0.25) * (5.0 * identity - normed) * 0.25


def left_finish(square, received):
    width = square.shape[-1]
    root_left = inverse_root(left_stat(square))
    whole = jnp.einsum("...ij,...jk->...ik", root_left, received, precision=lax.Precision.HIGHEST)
    return (whole * math.sqrt(width)).astype(jnp.bfloat16)


def precondition(blocks):
    root_right = inverse_root(right_stat(blocks))
    half = jnp.einsum(
        "...ij,...jk->...ik",
        blocks.astype(jnp.float32),
        root_right,
        precision=lax.Precision.HIGHEST,
    )
    return left_finish(blocks, half)


def place_block(buffer, result, row_start, col_start):
    return lax.dynamic_update_slice(buffer, result, (row_start, col_start))


def body(layer_input, output_grads, projection):
    width = BLOCK
    rows_own = layer_input.shape[1]
    gathered = lax.all_gather(output_grads, "owner", axis=1, tiled=True)
    section = gathered
    input_sum = jnp.einsum(
        "tc,rc->tr", section, gather_axes(projection, DP, 1), preferred_element_type=jnp.float32
    )
    grad_input = input_sum.astype(jnp.bfloat16)
    section = lax.slice_in_dim(gathered, 0, QW // lax.axis_size(DP) * lax.axis_size(DP), axis=1)
    query_local = lax.psum_scatter(
        jnp.einsum("tc,tr->cr", section, layer_input, preferred_element_type=jnp.float32).astype(
            jnp.bfloat16
        ),
        DP,
        scatter_dimension=0,
        tiled=True,
    )
    query_count = query_local.shape[0] // width
    row_count = rows_own // width
    shaped = query_local.reshape(query_count, width, row_count, width)
    squares = jnp.transpose(shaped, (2, 0, 3, 1)).reshape(row_count * query_count, width, width)
    updates = precondition(squares)
    update_query = jnp.transpose(
        updates.reshape(row_count, query_count, width, width), (0, 2, 1, 3)
    ).reshape(rows_own, query_count * width)
    kv_term = jnp.einsum(
        "tc,tr->cr", gathered[:, QW:], layer_input, preferred_element_type=jnp.float32
    )
    kv_grads = lax.psum(kv_term.astype(jnp.bfloat16), DP)
    kv_count = kv_grads.shape[0] // width
    total = row_count * kv_count
    index_dp = lax.axis_index(DP)
    buffer = jnp.zeros((rows_own, kv_grads.shape[0]), jnp.float32)
    empty_square = jnp.zeros((width, width), jnp.float32)
    number = 0 + index_dp
    valid = number < total
    clamped = jnp.minimum(number, total - 1)
    block_row = clamped // kv_count
    block_col = clamped % kv_count
    square = lax.dynamic_slice(kv_grads, (block_col * width, block_row * width), (width, width)).T
    square, row_start, col_start = (square, block_row * width, block_col * width)
    result = lax.cond(
        valid,
        lambda operand: precondition(operand).astype(jnp.float32),
        lambda operand: empty_square,
        square,
    )
    buffer = place_block(buffer, result, row_start, col_start)
    update_kv = sum_at_owner(buffer.astype(jnp.bfloat16), DP, 1).astype(jnp.bfloat16)
    return (grad_input, update_query, update_kv)


def solution(mesh):
    torus = Mesh(mesh.devices.reshape(4, 4, mesh.shape["owner"]), ("dp_0", "dp_1", "owner"))
    placed = (P(DP, "owner"), P(DP, "owner"), P("owner", DP))
    return jax.shard_map(
        body,
        mesh=torus,
        in_specs=placed,
        out_specs=(P(DP, "owner"), P("owner", DP), P("owner", DP)),
        check_vma=False,
    )
```

profile of v0, /device:TPU:10, one launch (start us, length us, event | category | flops | bytes accessed | tf_op | source)
XLA Modules:
  0.0 654.1 jit_solution(5530023113139257753)
XLA Ops:
  7.2 0.7 all-gather.4.cloned.1.call-update
  7.9 0.0 all-gather.6.cloned.1.call-start
  8.0 0.7 all-gather.6.cloned.1.call-update
  8.7 0.0 all-reduce.2.cloned.1.call-start
  8.7 89.6 %all-gather.4.cloned.1.call-done = bf16[256,10240]{1,0:T(8,128)(2,1)} async-done(((bf16[256,640]{1,0:T(8,128)(2,1)}), bf16[256,10240]{1,0:T(8,128)(2,1)}) %all-gather.4.cloned.1.call-update) | async-done | bytes 5242896 | tf_op jit(solution)/shard_map/all_gather | solution.py:75
  98.3 3.4 convolution_convert_fusion.1
  101.7 0.0 all-gather.8.cloned.1.call-start
  101.8 53.0 %all-gather.6.cloned.1.call-done = bf16[512,2560]{1,0:T(8,128)(2,1)} async-done(((bf16[512,640]{1,0:T(8,128)(2,1)}), bf16[512,2560]{1,0:T(8,128)(2,1)}) %all-gather.6.cloned.1.call-update) | async-done | bytes 2621456 | tf_op jit(solution)/shard_map/all_gather | solution.py:17
  154.7 0.0 reduce-scatter.2.cloned.1.call-start
  154.8 7.9 %convolution_convert_fusion = bf16[8192,512]{1,0:T(8,128)(2,1)} fusion(bf16[256,512]{1,0:T(8,128)(2,1)S(1)} %copy-done, bf16[256,10240]{1,0:T(8,128)(2,1)} %all-gather.4.cloned.1.call-done), kind=kOutput, calls=%fused_computation.31 | convolution fusion | flops 2151677952 | bytes 12845056 | tf_op jit(solution)/shard_map/tc,tr->cr/dot_general | solution.py:83
  162.7 163.7 %all-reduce.2.cloned.1.call-done = bf16[2048,512]{1,0:T(8,128)(2,1)} async-done(((bf16[2048,512]{1,0:T(8,128)(2,1)}), bf16[2048,512]{1,0:T(8,128)(2,1)}) %all-reduce.2.cloned.1.call-update) | async-done | bytes 2097168 | tf_op jit(solution)/shard_map/psum | solution.py:101
  326.5 1.1 dynamic-slice_bitcast_fusion
  327.5 0.1 conditional.1
  327.6 0.1 broadcast_in_dim.4
  327.8 2.4 copy.10
  330.2 56.7 %all_to_all.5 = bf16[16,512,128]{2,1,0:T(8,128)(2,1)S(1)} all-to-all(bf16[16,512,128]{2,1,0:T(8,128)(2,1)} %copy.10), channel_id=1, replica_groups=mesh['dp_0'=4,'dp_1'=4,'owner'=16] {'dp_0','dp_1'}, dimensions={0} | all-to-all | bytes 4194304 | tf_op jit(solution)/shard_map/all_to_all | solution.py:28
  386.8 1.0 reduce_sum.50
  387.8 63.1 %all-gather.8.cloned.1.call-done = bf16[512,10240]{1,0:T(8,128)(2,1)} async-done(((bf16[512,2560]{1,0:T(8,128)(2,1)}), bf16[512,10240]{1,0:T(8,128)(2,1)}) %all-gather.8.cloned.1.call-update) | async-done | bytes 10485776 | tf_op jit(solution)/shard_map/all_gather | solution.py:17
  450.9 9.2 %convolution_convert_fusion.2 = bf16[256,512]{1,0:T(8,128)(2,1)} fusion(bf16[256,10240]{1,0:T(8,128)(2,1)} %all-gather.4.cloned.1.call-done, bf16[512,10240]{1,0:T(8,128)(2,1)} %all-gather.8.cloned.1.call-done), kind=kOutput, calls=%fused_computation.38 | convolution fusion | flops 2684485632 | bytes 15990784 | tf_op jit(solution)/shard_map/tc,rc->tr/dot_general | solution.py:77
  460.1 176.1 %reduce-scatter.2.cloned.1.call-done = bf16[512,512]{1,0:T(8,128)(2,1)} async-done(((bf16[8192,512]{1,0:T(8,128)(2,1)}), bf16[512,512]{1,0:T(8,128)(2,1)}) %reduce-scatter.2.cloned.1.call-update) | async-done | bytes 524304 | tf_op jit(solution)/shard_map/reduce_scatter | solution.py:82
  636.2 2.4 multiply_reduce_fusion.2
  639.3 2.4 multiply_reduce_fusion.3
  642.5 2.3 fusion.34
  644.8 2.8 fusion.28
  (8 shorter events, 0.2 us)
Async XLA Ops:
  7.2 91.2 %copy-start = (bf16[256,512]{1,0:T(8,128)(2,1)S(1)}, bf16[256,512]{1,0:T(8,128)(2,1)}, u32[]{:S(2)}) copy-start(bf16[256,512]{1,0:T(8,128)(2,1)} %param.5) | copy-start | bytes 786436
  7.2 91.1 %all-gather.4.cloned.1.call-start = ((), (), s32[]{:S(2)}) async-start(), calls=%async_computation.2 | async-start | bytes 5570560 | tf_op jit(solution)/shard_map/all_gather | solution.py:75
  7.9 146.8 %all-gather.6.cloned.1.call-start = ((), (), s32[]{:S(2)}) async-start(), calls=%async_computation.3 | async-start | bytes 3276800 | tf_op jit(solution)/shard_map/all_gather | solution.py:17
  8.7 317.8 %all-reduce.2.cloned.1.call-start = ((), (), s32[]{:S(2)}) async-start(), calls=%async_computation.6 | async-start | bytes 4194304 | tf_op jit(solution)/shard_map/psum | solution.py:101
  101.7 349.2 %all-gather.8.cloned.1.call-start = ((), (), s32[]{:S(2)}) async-start(), calls=%async_computation.4 | async-start | bytes 13107200 | tf_op jit(solution)/shard_map/all_gather | solution.py:17
  154.7 481.4 %reduce-scatter.2.cloned.1.call-start = ((), (), s32[]{:S(2)}) async-start(), calls=%async_computation.5 | async-start | bytes 8912896 | tf_op jit(solution)/shard_map/reduce_scatter | solution.py:82
Sparse Core Ops, SparseCore 0:
  10.7 87.5 all-gather.3
  100.1 54.5 all-gather.5
  157.4 169.0 all-reduce.1
  328.1 122.7 all-gather.7
  453.3 182.8 reduce-scatter.1
where the time goes:
time: 657 us; the launch traced here: 654 us
  waiting for transfers between devices  547 us (83%)
  blocking collectives  56.7 us (9%)
  matrix products  30.3 us (5%)
  between operations  15.3 us (2%)
    reduce_scatter x1, waiting for transfers between devices, body(): lax.psum_scatter(jnp.einsum('tc,tr->cr', section, layer_input, preferred_...  176 us
    psum x1, waiting for transfers between devices, body(): kv_grads = lax.psum(kv_term.astype(jnp.bfloat16), DP)  164 us
    all_gather x2, waiting for transfers between devices, gather_axes(): whole = lax.all_gather(whole, axes[number], axis=dim, tiled=True)  116 us
    all_gather x1, waiting for transfers between devices, body(): gathered = lax.all_gather(output_grads, 'owner', axis=1, tiled=True)  89.6 us
    all_to_all x1, blocking collectives, sum_at_owner(): lax.all_to_all(split_up(shard, dim, devices), axis, 0, 0, tiled=True)  56.7 us
  transfers between devices with their start and end apart: 5, of which 5 were waited for; matrix products, arithmetic and copies ran while one was open for 4% of the time, Pallas kernels for 0%

commit v1 on v0

v1 whole, which is shorter than its diff:
```python
import functools
import math

import jax
import jax.numpy as jnp
from jax import lax
from jax.experimental import pallas as pl
from jax.experimental.pallas import tpu as pltpu
from jax.sharding import PartitionSpec as P

BLOCK = 512
UNIT = 128
SLOTS = 20
VMEM_LIMIT = 60 * 1024 * 1024
BF16 = jnp.bfloat16
F32 = jnp.float32


class Place:
    def __init__(self):
        dp = lax.axis_index("dp")
        owner = lax.axis_index("owner")
        self.x = dp // 4
        self.z = dp % 4
        self.zh = owner // 8
        self.y = (owner // 2) % 4
        self.c = owner % 2
        self.dp = dp
        self.owner = owner

    def at(self, x=None, z=None, zh=None, y=None, c=None):
        x = self.x if x is None else x
        z = self.z if z is None else z
        zh = self.zh if zh is None else zh
        y = self.y if y is None else y
        c = self.c if c is None else c
        return (x * 4 + z, zh * 8 + y * 2 + c)


def unit_of(z, slot):
    group = slot // 5
    step = slot % 5
    kv = step // 4
    return (1 - kv) * (16 * group + 4 * z + step) + kv * (64 + 4 * group + z)


def slot_of(unit):
    kv = unit // 64
    z = (1 - kv) * ((unit // 4) % 4) + kv * (unit % 4)
    slot = (1 - kv) * (5 * (unit // 16) + unit % 4) + kv * (5 * ((unit - 64 * kv) // 4) + 4)
    return z, slot


def remote(src, dst, send, recv, device):
    return pltpu.make_async_remote_copy(
        src_ref=src,
        dst_ref=dst,
        send_sem=send,
        recv_sem=recv,
        device_id=device,
        device_id_type=pl.DeviceIdType.MESH,
    )


def cols(slot):
    return pl.ds(pl.multiple_of(slot * UNIT, UNIT), UNIT)


def greet(devices):
    barrier = pltpu.get_barrier_semaphore()
    for device in devices:
        pl.semaphore_signal(barrier, inc=1, device_id=device, device_id_type=pl.DeviceIdType.MESH)
    pl.semaphore_wait(barrier, len(devices))


def gather_kernel(x_ref, g_ref, p_ref, xg, gd, pg, gs1, gs, gr, ps1, ps, pr, xs, xr):
    me = Place()
    tokens = g_ref.shape[0]
    rows = p_ref.shape[0]
    half = rows // 2
    devices = []
    for step in range(1, 8):
        far = (me.zh * 4 + me.z + step) % 8
        devices.append(me.at(z=far % 4, zh=far // 4))
    yp, ym = (me.y + 1) % 4, (me.y + 3) % 4
    xp, xm = (me.x + 1) % 4, (me.x + 3) % 4
    devices += [me.at(y=yp), me.at(y=ym), me.at(c=1 - me.c), me.at(x=xp), me.at(x=xm)]
    greet(devices)

    def mine(z):
        return pl.ds(pl.multiple_of(z * tokens, tokens), tokens)

    for k in range(5):
        q, slot = slot_of(5 * me.owner + k)
        src = g_ref.at[:, k * UNIT : (k + 1) * UNIT]
        dst = gd.at[mine(me.z), cols(slot)]
        for zh in range(2):
            here = jnp.logical_and(q == me.z, me.zh == zh)

            @pl.when(here)
            def _():
                pltpu.make_async_copy(src, dst, gr.at[slot, me.z]).start()

            @pl.when(jnp.logical_not(here))
            def _():
                remote(src, dst, gs1.at[k, zh], gr.at[slot, me.z], me.at(z=q, zh=zh)).start()

    for k in range(5):
        q, slot = slot_of(5 * me.dp + k)
        src = p_ref.at[:, k * UNIT : (k + 1) * UNIT]
        dst = pg.at[:, cols(slot)]

        @pl.when(q == me.z)
        def _():
            pltpu.make_async_copy(src, dst, pr.at[slot, 0]).start()

        @pl.when(q != me.z)
        def _():
            remote(src, dst, ps1.at[k], pr.at[slot, 0], me.at(z=q)).start()

    def x_send(src, origin, side):
        to = me.z + 1 if side == 0 else me.z - 1
        return remote(src, xg.at[mine(origin)], xs.at[side, origin], xr.at[origin], me.at(z=to))

    own_x = pltpu.make_async_copy(x_ref, xg.at[mine(me.z)], xr.at[me.z])
    own_x.start()

    @pl.when(me.z < 3)
    def _():
        x_send(x_ref, me.z, 0).start()

    @pl.when(me.z > 0)
    def _():
        x_send(x_ref, me.z, 1).start()

    own_x.wait()

    def x_step(step):
        low = me.z - step
        high = me.z + step

        @pl.when(low >= 0)
        def _():
            slot = jnp.maximum(low, 0)
            block = xg.at[mine(slot)]
            pltpu.make_async_copy(x_ref, block, xr.at[slot]).wait()

            @pl.when(me.z < 3)
            def _():
                x_send(block, slot, 0).start()

        @pl.when(high <= 3)
        def _():
            slot = jnp.minimum(high, 3)
            block = xg.at[mine(slot)]
            pltpu.make_async_copy(x_ref, block, xr.at[slot]).wait()

            @pl.when(me.z > 0)
            def _():
                x_send(block, slot, 1).start()

    def g_parts(slot):
        unit = unit_of(me.z, slot)
        dy = (me.y - (unit // 10) % 4 + 4) % 4
        ring = (unit // 5) % 2 == me.c
        whole = gd.at[:, cols(slot)]
        upper = gd.at[0 : 2 * tokens, cols(slot)]
        lower = gd.at[2 * tokens : 4 * tokens, cols(slot)]
        return dy, ring, whole, upper, lower

    def g_send(part, slot, way, index=0):
        device = (me.at(y=yp), me.at(y=ym), me.at(c=1 - me.c))[way]
        return remote(part, part, gs.at[slot, way], gr.at[slot, index], device)

    def g_wait(part, slot, index):
        pltpu.make_async_copy(part, part, gr.at[slot, index]).wait()

    def p_parts(slot):
        unit = unit_of(me.z, slot)
        dx = (me.x - unit // 20 + 4) % 4
        whole = pg.at[:, cols(slot)]
        upper = pg.at[0:half, cols(slot)]
        lower = pg.at[half:rows, cols(slot)]
        return dx, whole, upper, lower

    def p_send(part, slot, way, index=0):
        device = (me.at(x=xp), me.at(x=xm))[way]
        return remote(part, part, ps.at[slot, way], pr.at[slot, index], device)

    def p_wait(part, slot, index):
        pltpu.make_async_copy(part, part, pr.at[slot, index]).wait()

    @pl.loop(0, SLOTS)
    def _(slot):
        dy, ring, whole, upper, lower = g_parts(slot)

        @pl.when(jnp.logical_and(ring, dy == 0))
        def _():
            for t in range(4):
                g_wait(gd.at[t * tokens : (t + 1) * tokens, cols(slot)], slot, t)
            g_send(whole, slot, 0).start()
            g_send(whole, slot, 1).start()
            g_send(whole, slot, 2).start()

    @pl.loop(0, SLOTS)
    def _(slot):
        dx, whole, upper, lower = p_parts(slot)

        @pl.when(dx == 0)
        def _():
            p_wait(whole, slot, 0)
            p_send(whole, slot, 0).start()
            p_send(whole, slot, 1).start()

    x_step(1)

    @pl.loop(0, SLOTS)
    def _(slot):
        dy, ring, whole, upper, lower = g_parts(slot)

        @pl.when(jnp.logical_and(ring, dy == 1))
        def _():
            g_wait(whole, slot, 0)
            g_send(upper, slot, 0).start()
            g_send(whole, slot, 2).start()

        @pl.when(jnp.logical_and(ring, dy == 3))
        def _():
            g_wait(whole, slot, 0)
            g_send(lower, slot, 1, 1).start()
            g_send(whole, slot, 2).start()

    x_step(2)

    @pl.loop(0, SLOTS)
    def _(slot):
        dx, whole, upper, lower = p_parts(slot)

        @pl.when(dx == 1)
        def _():
            p_wait(whole, slot, 0)
            p_send(upper, slot, 0).start()

        @pl.when(dx == 3)
        def _():
            p_wait(whole, slot, 0)
            p_send(lower, slot, 1, 1).start()

    @pl.loop(0, SLOTS)
    def _(slot):
        dy, ring, whole, upper, lower = g_parts(slot)

        @pl.when(jnp.logical_and(ring, dy == 2))
        def _():
            g_wait(upper, slot, 0)
            g_wait(lower, slot, 1)
            g_send(whole, slot, 2).start()

    x_step(3)

    @pl.loop(0, SLOTS)
    def _(slot):
        dx, whole, upper, lower = p_parts(slot)

        @pl.when(dx == 2)
        def _():
            p_wait(upper, slot, 0)
            p_wait(lower, slot, 1)

    @pl.loop(0, SLOTS)
    def _(slot):
        dy, ring, whole, upper, lower = g_parts(slot)

        @pl.when(jnp.logical_not(ring))
        def _():
            g_wait(whole, slot, 0)

    for k in range(5):
        q, slot = slot_of(5 * me.owner + k)
        src = g_ref.at[:, k * UNIT : (k + 1) * UNIT]
        for zh in range(2):
            @pl.when(jnp.logical_not(jnp.logical_and(q == me.z, me.zh == zh)))
            def _():
                pltpu.make_async_copy(src, src, gs1.at[k, zh]).wait()

        q, slot = slot_of(5 * me.dp + k)
        psrc = p_ref.at[:, k * UNIT : (k + 1) * UNIT]

        @pl.when(q != me.z)
        def _():
            pltpu.make_async_copy(psrc, psrc, ps1.at[k]).wait()

    for origin in range(4):
        block = xg.at[origin * tokens : (origin + 1) * tokens]

        @pl.when(jnp.logical_and(origin <= me.z, me.z < 3))
        def _():
            pltpu.make_async_copy(block, block, xs.at[0, origin]).wait()

        @pl.when(jnp.logical_and(origin >= me.z, me.z > 0))
        def _():
            pltpu.make_async_copy(block, block, xs.at[1, origin]).wait()

    @pl.loop(0, SLOTS)
    def _(slot):
        dy, ring, whole, upper, lower = g_parts(slot)

        @pl.when(ring)
        def _():
            pltpu.make_async_copy(whole, whole, gs.at[slot, 2]).wait()

        @pl.when(jnp.logical_and(ring, dy == 0))
        def _():
            pltpu.make_async_copy(whole, whole, gs.at[slot, 0]).wait()
            pltpu.make_async_copy(whole, whole, gs.at[slot, 1]).wait()

        @pl.when(jnp.logical_and(ring, dy == 1))
        def _():
            pltpu.make_async_copy(upper, upper, gs.at[slot, 0]).wait()

        @pl.when(jnp.logical_and(ring, dy == 3))
        def _():
            pltpu.make_async_copy(lower, lower, gs.at[slot, 1]).wait()

        dx, whole, upper, lower = p_parts(slot)

        @pl.when(dx == 0)
        def _():
            pltpu.make_async_copy(whole, whole, ps.at[slot, 0]).wait()
            pltpu.make_async_copy(whole, whole, ps.at[slot, 1]).wait()

        @pl.when(dx == 1)
        def _():
            pltpu.make_async_copy(upper, upper, ps.at[slot, 0]).wait()

        @pl.when(dx == 3)
        def _():
            pltpu.make_async_copy(lower, lower, ps.at[slot, 1]).wait()


def exchange_kernel(w_ref, c_ref, wr, cr, fw, ws, wv, fs, fv, cs, cv, own):
    me = Place()
    width = wr.shape[2]
    half = wr.shape[1] // 2
    tokens = cr.shape[1]
    xp, xm, xo = (me.x + 1) % 4, (me.x + 3) % 4, (me.x + 2) % 4
    devices = [me.at(x=xp), me.at(x=xm)]
    for step in range(1, 4):
        devices.append(me.at(z=(me.z + step) % 4))
    greet(devices)

    def chunk(x):
        return pl.ds(pl.multiple_of(x * width, UNIT), width)

    first = [
        remote(w_ref.at[0:half, chunk(xo)], fw.at[0], fs.at[0], fv.at[0], me.at(x=xp)),
        remote(w_ref.at[half : 2 * half, chunk(xo)], fw.at[1], fs.at[1], fv.at[1], me.at(x=xm)),
    ]
    for copy in first:
        copy.start()
    direct = [
        remote(w_ref.at[:, chunk(xp)], wr.at[1], ws.at[0], wv.at[0], me.at(x=xp)),
        remote(w_ref.at[:, chunk(xm)], wr.at[3], ws.at[1], wv.at[1], me.at(x=xm)),
    ]
    for copy in direct:
        copy.start()
    for step in range(1, 4):
        to = (me.z + step) % 4
        copy = remote(
            c_ref.at[pl.ds(pl.multiple_of(to * tokens, tokens), tokens)],
            cr.at[step],
            cs.at[step],
            cv.at[step],
            me.at(z=to),
        )
        copy.start()
        direct.append(copy)
    mine = [
        pltpu.make_async_copy(w_ref.at[:, chunk(me.x)], wr.at[0], own.at[0]),
        pltpu.make_async_copy(
            c_ref.at[pl.ds(pl.multiple_of(me.z * tokens, tokens), tokens)], cr.at[0], own.at[1]
        ),
    ]
    for copy in mine:
        copy.start()
    first[0].wait_recv()
    second = [remote(fw.at[0], wr.at[2, 0:half], ws.at[2], wv.at[2], me.at(x=xp))]
    second[0].start()
    first[1].wait_recv()
    second.append(
        remote(fw.at[1], wr.at[2, half : 2 * half], ws.at[3], wv.at[3], me.at(x=xm))
    )
    second[1].start()
    for copy in first:
        copy.wait_send()
    for copy in mine + direct + second:
        copy.wait()


def spread_kernel(w_ref, out, send, recv, own):
    me = Place()
    devices = [me.at(z=(me.z + step) % 4) for step in range(1, 4)]
    greet(devices)
    mine = pltpu.make_async_copy(w_ref, out.at[0], own)
    mine.start()
    copies = [
        remote(w_ref, out.at[step], send.at[step], recv.at[step], devices[step - 1])
        for step in range(1, 4)
    ]
    for copy in copies:
        copy.start()
    mine.wait()
    for copy in copies:
        copy.wait()


def call(kernel, name, ident, outs, scratch, *operands):
    vmem = pl.BlockSpec(memory_space=pltpu.VMEM)
    return pl.pallas_call(
        kernel,
        name=name,
        out_shape=outs,
        in_specs=[pl.BlockSpec(memory_space=pl.ANY)] * len(operands),
        out_specs=jax.tree.map(lambda _: vmem, outs),
        scratch_shapes=scratch,
        compiler_params=pltpu.CompilerParams(
            collective_id=ident, has_side_effects=True, vmem_limit_bytes=VMEM_LIMIT
        ),
    )(*operands)


def dma(*shape):
    return pltpu.SemaphoreType.DMA(shape) if shape else pltpu.SemaphoreType.DMA


def split(value):
    high = value.astype(BF16)
    return high, (value - high.astype(F32)).astype(BF16)


def mm(a, b):
    return lax.dot_general(a, b, (((1,), (0,)), ((), ())), preferred_element_type=F32)


def update_of(left, target):
    width = left.shape[0]
    scale = math.sqrt(width) * jnp.sqrt(jnp.mean(left * left) + 1e-06)
    lh, ll = split(left / scale)
    once = mm(lh, target) + mm(ll, target)
    oh, ol = split(once)
    twice = mm(lh, oh) + mm(ll, oh) + mm(lh, ol)
    factor = math.sqrt(width) / 16.0 * lax.rsqrt(scale)
    return (factor * (25.0 * target.astype(F32) - 10.0 * once + twice)).astype(BF16)


def left_of(block):
    return lax.dot_general(block, block, (((1,), (1,)), ((), ())), preferred_element_type=F32)


def precondition_kernel(w_ref, kv_ref, uq, ukv):
    width = w_ref.shape[0]
    square = w_ref[:, 0:width]
    uq[...] = update_of(left_of(square), square)
    left = left_of(kv_ref[0])
    for part in range(1, 4):
        left += left_of(kv_ref[part])
    ukv[...] = update_of(left, kv_ref[0])


def body(layer_input, output_grads, projection):
    tokens, rows = layer_input.shape
    chunk = output_grads.shape[1]
    shape = jax.ShapeDtypeStruct
    xg, gd, pg = call(
        gather_kernel,
        "gather",
        0,
        (
            shape((4 * tokens, rows), BF16),
            shape((4 * tokens, SLOTS * UNIT), BF16),
            shape((rows, SLOTS * UNIT), BF16),
        ),
        [
            dma(5, 2),
            dma(SLOTS, 3),
            dma(SLOTS, 4),
            dma(5),
            dma(SLOTS, 2),
            dma(SLOTS, 2),
            dma(2, 4),
            dma(4),
        ],
        layer_input,
        output_grads,
        projection,
    )
    w_part = jnp.einsum("tr,tc->rc", xg, gd, preferred_element_type=F32).astype(BF16)
    c_part = jnp.einsum("tc,rc->tr", gd, pg, preferred_element_type=F32).astype(BF16)
    wr, cr = call(
        exchange_kernel,
        "exchange",
        1,
        (shape((4, rows, chunk), BF16), shape((4, tokens, rows), BF16)),
        [pltpu.VMEM((2, rows // 2, chunk), BF16), dma(4), dma(4), dma(2), dma(2), dma(4), dma(4), dma(2)],
        w_part,
        c_part,
    )
    grads = jnp.sum(wr.astype(F32), axis=0).astype(BF16)
    grad_input = jnp.sum(cr.astype(F32), axis=0).astype(BF16)
    kv = call(
        spread_kernel,
        "spread",
        2,
        shape((4, rows, UNIT), BF16),
        [dma(4), dma(4), dma()],
        grads[:, BLOCK:],
    )
    vmem = pl.BlockSpec(memory_space=pltpu.VMEM)
    update_query, update_kv = pl.pallas_call(
        precondition_kernel,
        name="precondition",
        out_shape=(shape((rows, BLOCK), BF16), shape((rows, UNIT), BF16)),
        in_specs=[vmem, vmem],
        out_specs=(vmem, vmem),
        compiler_params=pltpu.CompilerParams(vmem_limit_bytes=VMEM_LIMIT),
    )(grads, kv)
    return (grad_input, update_query, update_kv)


def solution(mesh):
    placed = (P("dp", "owner"), P("dp", "owner"), P("owner", "dp"))
    return jax.shard_map(
        body,
        mesh=mesh,
        in_specs=placed,
        out_specs=(P("dp", "owner"), P("owner", "dp"), P("owner", "dp")),
        check_vma=False,
    )
```

time: 657 us -> 154 us (0.23)
  waiting for transfers between devices: 547 us -> 0 us
  Pallas kernels: 0 us -> 136 us
  blocking collectives: 56.7 us -> 0 us
  matrix products: 30.3 us -> 11.7 us
  between operations: 15.3 us -> 0.69 us
    all_gather x3 -> x0, waiting for transfers between devices: 206 us -> none  [the longest x2 116 us: gather_axes(): whole = lax.all_gather(whole, axes[number], axis=dim, tiled=True)]
    reduce_scatter x1 -> x0, waiting for transfers between devices: 176 us -> none  [body(): lax.psum_scatter(jnp.einsum('tc,tr->cr', section, layer_input, preferred_...]
    psum x1 -> x0, waiting for transfers between devices: 164 us -> none  [body(): kv_grads = lax.psum(kv_term.astype(jnp.bfloat16), DP)]
    pallas_call x0 -> x4, Pallas kernels: none -> 136 us  [the longest x3 129 us: call(): pl.pallas_call(kernel, name=name, out_shape=outs, in_specs=[pl.BlockSpec(...]
    all_to_all x1 -> x0, blocking collectives: 56.7 us -> none  [sum_at_owner(): lax.all_to_all(split_up(shard, dim, devices), axis, 0, 0, tiled=True)]
    dot_general x7 -> x2, matrix products: 30.3 us -> 11.7 us  [the longest x1 7.41 us: body(): jnp.einsum('tc,rc->tr', gd, pg, preferred_element_type=F32).astype(BF16)]
  transfers between devices with their start and end apart: 5 -> 0, of which waited for: 5 -> 0; matrix products, arithmetic and copies ran while one was open for 4% -> 0% of each run, Pallas kernels for 0% -> 0%
where the time goes in v1:
time: 154 us; the launch traced here: 153 us
  Pallas kernels  136 us (88%)
  matrix products  11.7 us (8%)
  other arithmetic  4.63 us (3%)
    pallas_call x3, Pallas kernels, call(): pl.pallas_call(kernel, name=name, out_shape=outs, in_specs=[pl.BlockSpec(...  129 us
    dot_general x1, matrix products, body(): jnp.einsum('tc,rc->tr', gd, pg, preferred_element_type=F32).astype(BF16)  7.41 us
    pallas_call x1, Pallas kernels, body(): pl.pallas_call(precondition_kernel, name='precondition', out_shape=(shape...  6.7 us
    dot_general x1, matrix products, body(): jnp.einsum('tr,tc->rc', xg, gd, preferred_element_type=F32).astype(BF16)  4.28 us

profile of v1, /device:TPU:10, one launch (start us, length us, event | category | flops | bytes accessed | tf_op | source)
XLA Modules:
  0.0 153.5 jit_solution(12972688919509850365)
XLA Ops:
  0.6 79.3 %gather.1 = (bf16[1024,512]{1,0:T(8,128)(2,1)}, bf16[1024,2560]{1,0:T(8,128)(2,1)}, bf16[512,2560]{1,0:T(8,128)(2,1)}) custom-call(bf16[256,512]{1,0:T(8,128)(2,1)} %x_ref.1, bf16[256,640]{1,0:T(8,128)(2,1)} %g_ref.1, bf16[512,640]{1,0:T(8,128)(2,1)} %p_ref.1), custom_call_target="tpu_custom_call" | custom-call | tf_op jit(solution)/shard_map/gather/pallas_call | solution.py:419
  79.9 0.0 copy-start.1
  79.9 0.0 copy-start.2
  80.0 7.4 %convolution_convert_fusion.1.c_ref = bf16[1024,512]{1,0:T(8,128)(2,1)} fusion(bf16[1024,2560]{1,0:T(8,128)(2,1)} %get-tuple-element.11, bf16[512,2560]{1,0:T(8,128)(2,1)} %get-tuple-element.12), kind=kOutput, calls=%fused_computation.1 | convolution fusion | flops 2684878848 | bytes 8912896 | tf_op jit(solution)/shard_map/tc,rc->tr/dot_general | solution.py:498
  87.4 0.0 copy-done.1
  87.4 0.0 copy-done.2
  87.4 4.3 %convolution_convert_fusion.w_ref = bf16[512,2560]{1,0:T(8,128)(2,1)} fusion(bf16[1024,512]{1,0:T(8,128)(2,1)S(1)} %copy-done.2, bf16[1024,2560]{1,0:T(8,128)(2,1)S(1)} %copy-done.1), kind=kOutput, calls=%fused_computation | convolution fusion | flops 2685665280 | bytes 8912896 | tf_op jit(solution)/shard_map/tr,tc->rc/dot_general | solution.py:497
  91.7 37.4 %exchange.1 = (bf16[4,512,640]{2,1,0:T(8,128)(2,1)}, bf16[4,256,512]{2,1,0:T(8,128)(2,1)}) custom-call(bf16[512,2560]{1,0:T(8,128)(2,1)} %convolution_convert_fusion.w_ref, bf16[1024,512]{1,0:T(8,128)(2,1)} %convolution_convert_fusion.1.c_ref), custom_call_target="tpu_custom_call" | custom-call | tf_op jit(solution)/shard_map/exchange/pallas_call | solution.py:419
  129.0 2.2 %reduce_sum.24 = bf16[256,512]{1,0:T(8,128)(2,1)} reduce(bf16[4,256,512]{2,1,0:T(8,128)(2,1)} %get-tuple-element.13, bf16[]{:T(256)} %constant.3.clone.1), dimensions={0}, to_apply=%region_0.0 | reduce | flops 393216 | bytes 1310722 | tf_op jit(solution)/shard_map/reduce_sum | solution.py:509
  131.2 2.5 %reduce_sum.25.w_ref = bf16[512,640]{1,0:T(8,128)(2,1)S(1)} reduce(bf16[4,512,640]{2,1,0:T(8,128)(2,1)} %get-tuple-element.14, bf16[]{:T(256)} %constant.3.clone.1), dimensions={0}, to_apply=%region_1.0 | reduce | flops 983040 | bytes 3276802 | tf_op jit(solution)/shard_map/reduce_sum | solution.py:508
  133.7 0.0 copy-start
  133.7 0.7 slice.4.w_ref
  134.4 12.4 %spread.1.kv_ref = bf16[4,512,128]{2,1,0:T(8,128)(2,1)} custom-call(bf16[512,128]{1,0:T(8,128)(2,1)} %slice.4.w_ref), custom_call_target="tpu_custom_call" | custom-call | tf_op jit(solution)/shard_map/spread/pallas_call | solution.py:419
  146.8 0.0 copy-done
  146.8 6.7 %precondition.1 = (bf16[512,512]{1,0:T(8,128)(2,1)}, bf16[512,128]{1,0:T(8,128)(2,1)}) custom-call(bf16[512,640]{1,0:T(8,128)(2,1)} %copy-done, bf16[4,512,128]{2,1,0:T(8,128)(2,1)} %spread.1.kv_ref), custom_call_target="tpu_custom_call" | custom-call | tf_op jit(solution)/shard_map/precondition/pallas_call | solution.py:519
Async XLA Ops:
  79.9 7.4 %copy-start.1 = (bf16[1024,2560]{1,0:T(8,128)(2,1)S(1)}, bf16[1024,2560]{1,0:T(8,128)(2,1)}, u32[]{:S(2)}) copy-start(bf16[1024,2560]{1,0:T(8,128)(2,1)} %get-tuple-element.11) | copy-start | bytes 15728644
  79.9 7.4 %copy-start.2 = (bf16[1024,512]{1,0:T(8,128)(2,1)S(1)}, bf16[1024,512]{1,0:T(8,128)(2,1)}, u32[]{:S(2)}) copy-start(bf16[1024,512]{1,0:T(8,128)(2,1)} %get-tuple-element.10) | copy-start | bytes 3145732
  133.7 13.1 %copy-start = (bf16[512,640]{1,0:T(8,128)(2,1)}, bf16[512,640]{1,0:T(8,128)(2,1)S(1)}, u32[]{:S(2)}) copy-start(bf16[512,640]{1,0:T(8,128)(2,1)S(1)} %reduce_sum.25.w_ref) | copy-start | bytes 1966084

commit v2 on v1

v2 whole, which is shorter than its diff:
```python
import math

import jax
import jax.numpy as jnp
from jax import lax
from jax.experimental import pallas as pl
from jax.experimental.pallas import tpu as pltpu
from jax.sharding import PartitionSpec as P

BLOCK = 512
UNIT = 128
SLOTS = 20
VMEM_LIMIT = 60 * 1024 * 1024
BF16 = jnp.bfloat16
F32 = jnp.float32


class Place:
    def __init__(self):
        dp = lax.axis_index("dp")
        owner = lax.axis_index("owner")
        self.x = dp // 4
        self.z = dp % 4
        self.zh = owner // 8
        self.y = (owner // 2) % 4
        self.c = owner % 2
        self.dp = dp
        self.owner = owner

    def at(self, x=None, z=None, zh=None, y=None, c=None):
        x = self.x if x is None else x
        z = self.z if z is None else z
        zh = self.zh if zh is None else zh
        y = self.y if y is None else y
        c = self.c if c is None else c
        return (x * 4 + z, zh * 8 + y * 2 + c)


def unit_of(z, slot):
    group = slot // 5
    step = slot % 5
    kv = step // 4
    return (1 - kv) * (16 * group + 4 * z + step) + kv * (64 + 4 * group + z)


def slot_of(unit):
    kv = unit // 64
    z = (1 - kv) * ((unit // 4) % 4) + kv * (unit % 4)
    slot = (1 - kv) * (5 * (unit // 16) + unit % 4) + kv * (5 * ((unit - 64 * kv) // 4) + 4)
    return z, slot


def remote(src, dst, send, recv, device):
    return pltpu.make_async_remote_copy(
        src_ref=src,
        dst_ref=dst,
        send_sem=send,
        recv_sem=recv,
        device_id=device,
        device_id_type=pl.DeviceIdType.MESH,
    )


def cols(slot):
    return pl.ds(pl.multiple_of(slot * UNIT, UNIT), UNIT)


def greet(devices):
    barrier = pltpu.get_barrier_semaphore()
    for device in devices:
        pl.semaphore_signal(barrier, inc=1, device_id=device, device_id_type=pl.DeviceIdType.MESH)
    pl.semaphore_wait(barrier, len(devices))


def fused_kernel(
    x_ref, g_ref, p_ref, out_c, out_q, out_kv,
    xg, xt, gd, pg, kp, qp, kf, qf, kl, kr, ql, qr, kv, cp, ca, cb,
    gs1, gs, gr, ps1, ps, pr, xs, xr,
    fks, fkr, fqs, fqr, ks, kvr, qs, qvr, ss, sr, cs, crv,
):
    me = Place()
    tokens = g_ref.shape[0]
    rows = p_ref.shape[0]
    half = rows // 2
    yp, ym, yo = (me.y + 1) % 4, (me.y + 3) % 4, (me.y + 2) % 4
    xp, xm, xo = (me.x + 1) % 4, (me.x + 3) % 4, (me.x + 2) % 4
    devices = []
    for step in range(1, 8):
        far = (me.zh * 4 + me.z + step) % 8
        devices.append(me.at(z=far % 4, zh=far // 4))
    devices += [me.at(y=yp), me.at(y=ym), me.at(c=1 - me.c), me.at(x=xp), me.at(x=xm)]
    greet(devices)

    def mine(z):
        return pl.ds(pl.multiple_of(z * tokens, tokens), tokens)

    def wait_for(part, sem):
        pltpu.make_async_copy(part, part, sem).wait()

    for k in range(5):
        q, slot = slot_of(5 * me.owner + k)
        src = g_ref.at[:, k * UNIT : (k + 1) * UNIT]
        dst = gd.at[mine(me.z), cols(slot)]
        for zh in range(2):
            here = jnp.logical_and(q == me.z, me.zh == zh)

            @pl.when(here)
            def _():
                pltpu.make_async_copy(src, dst, gr.at[slot, me.z]).start()

            @pl.when(jnp.logical_not(here))
            def _():
                remote(src, dst, gs1.at[k, zh], gr.at[slot, me.z], me.at(z=q, zh=zh)).start()

    for k in range(5):
        q, slot = slot_of(5 * me.dp + k)
        src = p_ref.at[:, k * UNIT : (k + 1) * UNIT]
        dst = pg.at[:, cols(slot)]

        @pl.when(q == me.z)
        def _():
            pltpu.make_async_copy(src, dst, pr.at[slot, 0]).start()

        @pl.when(q != me.z)
        def _():
            remote(src, dst, ps1.at[k], pr.at[slot, 0], me.at(z=q)).start()

    def x_send(src, origin, side):
        to = me.z + 1 if side == 0 else me.z - 1
        return remote(src, xg.at[mine(origin)], xs.at[side, origin], xr.at[origin], me.at(z=to))

    own_x = pltpu.make_async_copy(x_ref, xg.at[mine(me.z)], xr.at[me.z])
    own_x.start()

    @pl.when(me.z < 3)
    def _():
        x_send(x_ref, me.z, 0).start()

    @pl.when(me.z > 0)
    def _():
        x_send(x_ref, me.z, 1).start()

    own_x.wait()

    def x_step(step):
        low = me.z - step
        high = me.z + step

        @pl.when(low >= 0)
        def _():
            slot = jnp.maximum(low, 0)
            block = xg.at[mine(slot)]
            wait_for(block, xr.at[slot])

            @pl.when(me.z < 3)
            def _():
                x_send(block, slot, 0).start()

        @pl.when(high <= 3)
        def _():
            slot = jnp.minimum(high, 3)
            block = xg.at[mine(slot)]
            wait_for(block, xr.at[slot])

            @pl.when(me.z > 0)
            def _():
                x_send(block, slot, 1).start()

    def g_unit(y, c, zh, k):
        q, slot = slot_of(5 * (8 * zh + 2 * y + c) + k)
        whole = gd.at[:, cols(slot)]
        upper = gd.at[0 : 2 * tokens, cols(slot)]
        lower = gd.at[2 * tokens : 4 * tokens, cols(slot)]
        return q == me.z, slot, whole, upper, lower

    def g_send(part, slot, way, index=0):
        device = (me.at(y=yp), me.at(y=ym), me.at(c=1 - me.c))[way]
        return remote(part, part, gs.at[slot, way], gr.at[slot, index], device)

    def p_unit(x, z, k):
        q, slot = slot_of(5 * (4 * x + z) + k)
        whole = pg.at[:, cols(slot)]
        upper = pg.at[0:half, cols(slot)]
        lower = pg.at[half:rows, cols(slot)]
        return q == me.z, slot, whole, upper, lower

    def p_send(part, slot, way, index=0):
        device = (me.at(x=xp), me.at(x=xm))[way]
        return remote(part, part, ps.at[slot, way], pr.at[slot, index], device)

    def g_origin(k, waiting):
        for zh in range(2):
            ok, slot, whole, upper, lower = g_unit(me.y, me.c, zh, k)

            @pl.when(ok)
            def _():
                if waiting:
                    for way in range(3):
                        wait_for(whole, gs.at[slot, way])
                else:
                    for t in range(4):
                        wait_for(gd.at[t * tokens : (t + 1) * tokens, cols(slot)], gr.at[slot, t])
                    for way in range(3):
                        g_send(whole, slot, way).start()

    def g_next(k, waiting):
        for zh in range(2):
            for side, y in ((0, ym), (1, yp)):
                ok, slot, whole, upper, lower = g_unit(y, me.c, zh, k)
                part = upper if side == 0 else lower

                @pl.when(ok)
                def _():
                    if waiting:
                        wait_for(part, gs.at[slot, side])
                        wait_for(whole, gs.at[slot, 2])
                    else:
                        wait_for(whole, gr.at[slot, 0])
                        g_send(part, slot, side, side).start()
                        g_send(whole, slot, 2).start()

    def g_last(k, waiting):
        for zh in range(2):
            ok, slot, whole, upper, lower = g_unit(yo, me.c, zh, k)

            @pl.when(ok)
            def _():
                if waiting:
                    wait_for(whole, gs.at[slot, 2])
                else:
                    wait_for(upper, gr.at[slot, 0])
                    wait_for(lower, gr.at[slot, 1])
                    g_send(whole, slot, 2).start()

    def g_sibling(k):
        for zh in range(2):
            for y in range(4):
                ok, slot, whole, upper, lower = g_unit(y, 1 - me.c, zh, k)

                @pl.when(ok)
                def _():
                    wait_for(whole, gr.at[slot, 0])

    def p_origin(k, waiting):
        for z in range(4):
            ok, slot, whole, upper, lower = p_unit(me.x, z, k)

            @pl.when(ok)
            def _():
                if waiting:
                    for way in range(2):
                        wait_for(whole, ps.at[slot, way])
                else:
                    wait_for(whole, pr.at[slot, 0])
                    for way in range(2):
                        p_send(whole, slot, way).start()

    def p_next(k, waiting):
        for z in range(4):
            for side, x in ((0, xm), (1, xp)):
                ok, slot, whole, upper, lower = p_unit(x, z, k)
                part = upper if side == 0 else lower

                @pl.when(ok)
                def _():
                    if waiting:
                        wait_for(part, ps.at[slot, side])
                    else:
                        wait_for(whole, pr.at[slot, 0])
                        p_send(part, slot, side, side).start()

    def p_last(k):
        for z in range(4):
            ok, slot, whole, upper, lower = p_unit(xo, z, k)

            @pl.when(ok)
            def _():
                wait_for(upper, pr.at[slot, 0])
                wait_for(lower, pr.at[slot, 1])

    @pl.loop(0, 5)
    def _(k):
        g_origin(k, False)
        p_origin(k, False)

    x_step(1)

    @pl.loop(0, 5)
    def _(k):
        g_next(k, False)
        p_next(k, False)

    x_step(2)

    @pl.loop(0, 5)
    def _(k):
        g_last(k, False)

    x_step(3)

    @pl.loop(0, 4)
    def _(t):
        xt[:, mine(t)] = xg[mine(t), :].T

    @pl.loop(0, 5)
    def _(k):
        g_sibling(k)

    def w_dot(x, first, count):
        at = pl.ds(pl.multiple_of((5 * x + first) * UNIT, UNIT), count * UNIT)
        return mm(xt[...], gd[:, at]).astype(BF16)

    kp[0] = w_dot(xo, 4, 1)
    kp[1] = w_dot(xp, 4, 1)
    kp[2] = w_dot(xm, 4, 1)
    plus, minus = me.at(x=xp), me.at(x=xm)
    raw_k = [
        remote(kp.at[0, 0:half], kf.at[0], fks.at[0], fkr.at[0], plus),
        remote(kp.at[0, half:rows], kf.at[1], fks.at[1], fkr.at[1], minus),
    ]
    own_k = [
        remote(kp.at[1, half:rows], kl.at[half:rows], ks.at[0], kvr.at[0], plus),
        remote(kp.at[2, 0:half], kr.at[0:half], ks.at[1], kvr.at[1], minus),
    ]
    for copy in raw_k + own_k:
        copy.start()
    qp[0] = w_dot(xo, 0, 4)
    raw_q = [
        remote(qp.at[0, 0:half], qf.at[0], fqs.at[0], fqr.at[0], plus),
        remote(qp.at[0, half:rows], qf.at[1], fqs.at[1], fqr.at[1], minus),
    ]
    for copy in raw_q:
        copy.start()
    qp[1] = w_dot(xp, 0, 4)
    qp[2] = w_dot(xm, 0, 4)
    own_q = [
        remote(qp.at[1, half:rows], ql.at[half:rows], qs.at[0], qvr.at[0], plus),
        remote(qp.at[2, 0:half], qr.at[0:half], qs.at[1], qvr.at[1], minus),
    ]
    for copy in own_q:
        copy.start()

    def add(a, b):
        return (a.astype(F32) + b.astype(F32)).astype(BF16)

    for copy in raw_k:
        copy.wait_recv()
    kf[0] = add(kf[0], kp[1, 0:half])
    kf[1] = add(kf[1], kp[2, half:rows])
    sum_k = [
        remote(kf.at[0], kl.at[0:half], ks.at[2], kvr.at[2], plus),
        remote(kf.at[1], kr.at[half:rows], ks.at[3], kvr.at[3], minus),
    ]
    for copy in sum_k:
        copy.start()

    @pl.loop(0, 5)
    def _(k):
        p_last(k)

    def c_dot(d):
        block = gd[d * tokens : (d + 1) * tokens, :]
        cp[d] = lax.dot_general(
            block, pg[...], (((1,), (1,)), ((), ())), preferred_element_type=F32
        ).astype(BF16)

    def c_copy(d, side):
        buffer = ca if side == 0 else cb
        to = jnp.minimum(me.z + 1, 3) if side == 0 else jnp.maximum(me.z - 1, 0)
        return remote(cp.at[d], buffer.at[d], cs.at[d], crv.at[side, d], me.at(z=to))

    def c_step(step):
        d = 3 - step

        @pl.when(me.z < d)
        def _():
            @pl.when(me.z > 0)
            def _():
                wait_for(ca.at[d], crv.at[0, d])
                cp[d] = add(cp[d], ca[d])

            c_copy(d, 0).start()

        e = step

        @pl.when(me.z > e)
        def _():
            @pl.when(me.z < 3)
            def _():
                wait_for(cb.at[e], crv.at[1, e])
                cp[e] = add(cp[e], cb[e])

            c_copy(e, 1).start()

    c_dot(3)
    c_dot(0)
    c_step(0)

    for copy in raw_q:
        copy.wait_recv()
    qf[0] = add(qf[0], qp[1, 0:half])
    qf[1] = add(qf[1], qp[2, half:rows])
    sum_q = [
        remote(qf.at[0], ql.at[0:half], qs.at[2], qvr.at[2], plus),
        remote(qf.at[1], qr.at[half:rows], qs.at[3], qvr.at[3], minus),
    ]
    for copy in sum_q:
        copy.start()

    c_dot(2)
    c_dot(1)
    c_step(1)

    kw = mm(xt[...], gd[:, pl.ds(pl.multiple_of((5 * me.x + 4) * UNIT, UNIT), UNIT)])
    for copy in own_k + sum_k:
        copy.wait_recv()
    kv[me.z] = (kw + kl[...].astype(F32) + kr[...].astype(F32)).astype(BF16)

    def kv_send(origin, side):
        to = me.z + 1 if side == 0 else me.z - 1
        return remote(kv.at[origin], kv.at[origin], ss.at[side, origin], sr.at[origin], me.at(z=to))

    @pl.when(me.z < 3)
    def _():
        kv_send(me.z, 0).start()

    @pl.when(me.z > 0)
    def _():
        kv_send(me.z, 1).start()

    c_step(2)
    qw = mm(xt[...], gd[:, pl.ds(pl.multiple_of(5 * me.x * UNIT, UNIT), 4 * UNIT)])

    for step in range(1, 4):
        low = me.z - step
        high = me.z + step

        @pl.when(low >= 0)
        def _():
            slot = jnp.maximum(low, 0)
            wait_for(kv.at[slot], sr.at[slot])

            @pl.when(me.z < 3)
            def _():
                kv_send(slot, 0).start()

        @pl.when(high <= 3)
        def _():
            slot = jnp.minimum(high, 3)
            wait_for(kv.at[slot], sr.at[slot])

            @pl.when(me.z > 0)
            def _():
                kv_send(slot, 1).start()

    gram = left_of(kv[0])
    for part in range(1, 4):
        gram += left_of(kv[part])
    out_kv[...] = update_of(gram, kv[me.z])

    for copy in own_q + sum_q:
        copy.wait_recv()
    square = (qw + ql[...].astype(F32) + qr[...].astype(F32)).astype(BF16)
    out_q[...] = update_of(left_of(square), square)

    for d in range(4):
        @pl.when(me.z == d)
        def _():
            total = cp[d].astype(F32)
            if d > 0:
                wait_for(ca.at[d], crv.at[0, d])
                total += ca[d].astype(F32)
            if d < 3:
                wait_for(cb.at[d], crv.at[1, d])
                total += cb[d].astype(F32)
            out_c[...] = total.astype(BF16)

    for k in range(5):
        q, slot = slot_of(5 * me.owner + k)
        src = g_ref.at[:, k * UNIT : (k + 1) * UNIT]
        for zh in range(2):
            @pl.when(jnp.logical_not(jnp.logical_and(q == me.z, me.zh == zh)))
            def _():
                wait_for(src, gs1.at[k, zh])

        q, slot = slot_of(5 * me.dp + k)
        psrc = p_ref.at[:, k * UNIT : (k + 1) * UNIT]

        @pl.when(q != me.z)
        def _():
            wait_for(psrc, ps1.at[k])

    @pl.loop(0, 5)
    def _(k):
        g_origin(k, True)
        g_next(k, True)
        g_last(k, True)
        p_origin(k, True)
        p_next(k, True)

    for origin in range(4):
        block = xg.at[origin * tokens : (origin + 1) * tokens]

        @pl.when(jnp.logical_and(origin <= me.z, me.z < 3))
        def _():
            wait_for(block, xs.at[0, origin])
            wait_for(kv.at[origin], ss.at[0, origin])

        @pl.when(jnp.logical_and(origin >= me.z, me.z > 0))
        def _():
            wait_for(block, xs.at[1, origin])
            wait_for(kv.at[origin], ss.at[1, origin])

        @pl.when(me.z != origin)
        def _():
            wait_for(cp.at[origin], cs.at[origin])

    for copy in raw_k + own_k + sum_k + raw_q + own_q + sum_q:
        copy.wait_send()


def dma(*shape):
    return pltpu.SemaphoreType.DMA(shape)


def split(value):
    high = value.astype(BF16)
    return high, (value - high.astype(F32)).astype(BF16)


def mm(a, b):
    return lax.dot_general(a, b, (((1,), (0,)), ((), ())), preferred_element_type=F32)


def update_of(left, target):
    width = left.shape[0]
    scale = math.sqrt(width) * jnp.sqrt(jnp.mean(left * left) + 1e-06)
    lh, ll = split(left * (1.0 / scale))
    once = mm(lh, target) + mm(ll, target)
    oh, ol = split(once)
    twice = mm(lh, oh) + mm(ll, oh) + mm(lh, ol)
    factor = math.sqrt(width) / 16.0 * lax.rsqrt(scale)
    return (factor * (25.0 * target.astype(F32) - 10.0 * once + twice)).astype(BF16)


def left_of(block):
    return lax.dot_general(block, block, (((1,), (1,)), ((), ())), preferred_element_type=F32)


def body(layer_input, output_grads, projection):
    tokens, rows = layer_input.shape
    half = rows // 2
    shape = jax.ShapeDtypeStruct
    vmem = pl.BlockSpec(memory_space=pltpu.VMEM)

    def space(*dims):
        return pltpu.VMEM(dims, BF16)

    return pl.pallas_call(
        fused_kernel,
        name="fused",
        out_shape=(
            shape((tokens, rows), BF16),
            shape((rows, BLOCK), BF16),
            shape((rows, UNIT), BF16),
        ),
        in_specs=[pl.BlockSpec(memory_space=pl.ANY)] * 3,
        out_specs=(vmem, vmem, vmem),
        scratch_shapes=[
            space(4 * tokens, rows),
            space(rows, 4 * tokens),
            space(4 * tokens, SLOTS * UNIT),
            space(rows, SLOTS * UNIT),
            space(3, rows, UNIT),
            space(3, rows, BLOCK),
            space(2, half, UNIT),
            space(2, half, BLOCK),
            space(rows, UNIT),
            space(rows, UNIT),
            space(rows, BLOCK),
            space(rows, BLOCK),
            space(4, rows, UNIT),
            space(4, tokens, rows),
            space(4, tokens, rows),
            space(4, tokens, rows),
            dma(5, 2),
            dma(SLOTS, 3),
            dma(SLOTS, 4),
            dma(5),
            dma(SLOTS, 2),
            dma(SLOTS, 2),
            dma(2, 4),
            dma(4),
            dma(2),
            dma(2),
            dma(2),
            dma(2),
            dma(4),
            dma(4),
            dma(4),
            dma(4),
            dma(2, 4),
            dma(4),
            dma(4),
            dma(2, 4),
        ],
        compiler_params=pltpu.CompilerParams(
            collective_id=0, has_side_effects=True, vmem_limit_bytes=VMEM_LIMIT
        ),
    )(layer_input, output_grads, projection)


def solution(mesh):
    placed = (P("dp", "owner"), P("dp", "owner"), P("owner", "dp"))
    return jax.shard_map(
        body,
        mesh=mesh,
        in_specs=placed,
        out_specs=(P("dp", "owner"), P("owner", "dp"), P("owner", "dp")),
        check_vma=False,
    )
```

time: 154 us -> 129 us (0.84)
  matrix products: 11.7 us -> 0 us
  Pallas kernels: 136 us -> 125 us
  other arithmetic: 4.63 us -> 0 us
  local copies, waits for them, and re-layouts: 0.71 us -> 3.41 us
    dot_general x2 -> x0, matrix products: 11.7 us -> none  [the longest x1 7.41 us: body(): jnp.einsum('tc,rc->tr', gd, pg, preferred_element_type=F32).astype(BF16)]
    pallas_call x4 -> x1, Pallas kernels: 136 us -> 125 us  [body(): pl.pallas_call(fused_kernel, name='fused', out_shape=(shape((tokens, rows...]
    reduce_sum x2 -> x0, other arithmetic: 4.63 us -> none  [the longest x1 2.47 us: body(): grads = jnp.sum(wr.astype(F32), axis=0).astype(BF16)]
    unnamed x6 -> x7, local copies, waits for them, and re-layouts: 0.01 us -> 3.41 us
where the time goes in v2:
time: 129 us
  Pallas kernels  125 us (97%)
  local copies, waits for them, and re-layouts  3.41 us (3%)
    pallas_call x1, Pallas kernels, body(): pl.pallas_call(fused_kernel, name='fused', out_shape=(shape((tokens, rows...  125 us
    unnamed x7, local copies, waits for them, and re-layouts  3.41 us

profile of v2, /device:TPU:10, one launch (start us, length us, event | category | flops | bytes accessed | tf_op | source)
XLA Modules:
  0.0 128.7 jit_solution(5363094525456681366)
XLA Ops:
  0.6 124.6 %fused.1 = (bf16[256,512]{1,0:T(8,128)(2,1)}, bf16[512,512]{1,0:T(8,128)(2,1)}, bf16[512,128]{1,0:T(8,128)(2,1)}) custom-call(bf16[256,512]{1,0:T(8,128)(2,1)} %x_ref.1, bf16[256,640]{1,0:T(8,128)(2,1)} %g_ref.1, bf16[512,640]{1,0:T(8,128)(2,1)} %p_ref.1), custom_call_target="tpu_custom_call" | custom-call | tf_op jit(solution)/shard_map/fused/pallas_call | solution.py:559
  125.3 0.0 copy-start
  125.3 1.7 %copy.9 = bf16[256,512]{1,0:T(8,128)(2,1)} copy(bf16[256,512]{1,0:T(8,128)(2,1)} %get-tuple-element.6) | data formatting | bytes 524288
  127.0 0.0 copy-done
  127.0 0.0 copy-start.1
  127.0 0.8 copy.10
  127.8 0.2 copy-done.1
  128.0 0.7 copy.11
Async XLA Ops:
  125.3 1.7 %copy-start = (bf16[512,512]{1,0:T(8,128)(2,1)S(1)}, bf16[512,512]{1,0:T(8,128)(2,1)}, u32[]{:S(2)}) copy-start(bf16[512,512]{1,0:T(8,128)(2,1)} %get-tuple-element.7) | copy-start | bytes 1572868
  127.0 1.0 copy-start.1

commit v3 on v2

--- a/solution.py
+++ b/solution.py
@@ -19,11 +19,11 @@
     def __init__(self):
         dp = lax.axis_index("dp")
         owner = lax.axis_index("owner")
-        self.x = dp // 4
-        self.z = dp % 4
-        self.zh = owner // 8
-        self.y = (owner // 2) % 4
-        self.c = owner % 2
+        self.x = dp >> 2
+        self.z = dp & 3
+        self.zh = owner >> 3
+        self.y = (owner >> 1) & 3
+        self.c = owner & 1
         self.dp = dp
         self.owner = owner
 
@@ -44,9 +44,12 @@
 
 
 def slot_of(unit):
-    kv = unit // 64
-    z = (1 - kv) * ((unit // 4) % 4) + kv * (unit % 4)
-    slot = (1 - kv) * (5 * (unit // 16) + unit % 4) + kv * (5 * ((unit - 64 * kv) // 4) + 4)
+    kv = unit >> 6
+    group = unit >> 2
+    low = unit - (group << 2)
+    rest = group & 3
+    z = rest + kv * (low - rest)
+    slot = 5 * (unit >> 4) + low + kv * (5 * (group - 16) + 4 - 5 * (unit >> 4) - low)
     return z, slot
 
 
@@ -281,20 +284,20 @@
     @pl.loop(0, 5)
     def _(k):
         g_origin(k, False)
-        p_origin(k, False)
-
-    x_step(1)
 
     @pl.loop(0, 5)
     def _(k):
+        p_origin(k, False)
         g_next(k, False)
-        p_next(k, False)
-
-    x_step(2)
+
+    x_step(1)
 
     @pl.loop(0, 5)
     def _(k):
+        p_next(k, False)
         g_last(k, False)
+
+    x_step(2)
 
     x_step(3)
 
@@ -306,13 +309,25 @@
     def _(k):
         g_sibling(k)
 
+    @pl.loop(0, 5)
+    def _(k):
+        p_last(k)
+
     def w_dot(x, first, count):
         at = pl.ds(pl.multiple_of((5 * x + first) * UNIT, UNIT), count * UNIT)
-        return mm(xt[...], gd[:, at]).astype(BF16)
-
-    kp[0] = w_dot(xo, 4, 1)
-    kp[1] = w_dot(xp, 4, 1)
-    kp[2] = w_dot(xm, 4, 1)
+        return mm(xt[...], gd[:, at])
+
+    def c_dot(d):
+        cp[d] = lax.dot_general(
+            gd[mine(d), :], pg[...], (((1,), (1,)), ((), ())), preferred_element_type=F32
+        ).astype(BF16)
+
+    def add(a, b):
+        return (a.astype(F32) + b.astype(F32)).astype(BF16)
+
+    kp[0] = w_dot(xo, 4, 1).astype(BF16)
+    kp[1] = w_dot(xp, 4, 1).astype(BF16)
+    kp[2] = w_dot(xm, 4, 1).astype(BF16)
     plus, minus = me.at(x=xp), me.at(x=xm)
     raw_k = [
         remote(kp.at[0, 0:half], kf.at[0], fks.at[0], fkr.at[0], plus),
@@ -324,25 +339,27 @@
     ]
     for copy in raw_k + own_k:
         copy.start()
-    qp[0] = w_dot(xo, 0, 4)
+    qp[0] = w_dot(xo, 0, 4).astype(BF16)
     raw_q = [
         remote(qp.at[0, 0:half], qf.at[0], fqs.at[0], fqr.at[0], plus),
         remote(qp.at[0, half:rows], qf.at[1], fqs.at[1], fqr.at[1], minus),
     ]
     for copy in raw_q:
         copy.start()
-    qp[1] = w_dot(xp, 0, 4)
-    qp[2] = w_dot(xm, 0, 4)
-    own_q = [
-        remote(qp.at[1, half:rows], ql.at[half:rows], qs.at[0], qvr.at[0], plus),
-        remote(qp.at[2, 0:half], qr.at[0:half], qs.at[1], qvr.at[1], minus),
-    ]
-    for copy in own_q:
+
+    odd = me.z % 2
+    near = me.at(z=me.z + 1 - 2 * odd)
+    away = (me.z + 2) % 4
+    c_near = []
+    for part in range(2):
+        d = 1 - odd + 2 * part
+        c_dot(d)
+        copy = remote(cp.at[d], ca.at[part], cs.at[part], crv.at[part], near)
         copy.start()
-
-    def add(a, b):
-        return (a.astype(F32) + b.astype(F32)).astype(BF16)
-
+        c_near.append(copy)
+
+    qp[1] = w_dot(xp, 0, 4).astype(BF16)
+    qp[2] = w_dot(xm, 0, 4).astype(BF16)
     for copy in raw_k:
         copy.wait_recv()
     kf[0] = add(kf[0], kp[1, 0:half])
@@ -351,51 +368,14 @@
         remote(kf.at[0], kl.at[0:half], ks.at[2], kvr.at[2], plus),
         remote(kf.at[1], kr.at[half:rows], ks.at[3], kvr.at[3], minus),
     ]
-    for copy in sum_k:
+    own_q = [
+        remote(qp.at[1, half:rows], ql.at[half:rows], qs.at[0], qvr.at[0], plus),
+        remote(qp.at[2, 0:half], qr.at[0:half], qs.at[1], qvr.at[1], minus),
+    ]
+    for copy in sum_k + own_q:
         copy.start()
-
-    @pl.loop(0, 5)
-    def _(k):
-        p_last(k)
-
-    def c_dot(d):
-        block = gd[d * tokens : (d + 1) * tokens, :]
-        cp[d] = lax.dot_general(
-            block, pg[...], (((1,), (1,)), ((), ())), preferred_element_type=F32
-        ).astype(BF16)
-
-    def c_copy(d, side):
-        buffer = ca if side == 0 else cb
-        to = jnp.minimum(me.z + 1, 3) if side == 0 else jnp.maximum(me.z - 1, 0)
-        return remote(cp.at[d], buffer.at[d], cs.at[d], crv.at[side, d], me.at(z=to))
-
-    def c_step(step):
-        d = 3 - step
-
-        @pl.when(me.z < d)
-        def _():
-            @pl.when(me.z > 0)
-            def _():
-                wait_for(ca.at[d], crv.at[0, d])
-                cp[d] = add(cp[d], ca[d])
-
-            c_copy(d, 0).start()
-
-        e = step
-
-        @pl.when(me.z > e)
-        def _():
-            @pl.when(me.z < 3)
-            def _():
-                wait_for(cb.at[e], crv.at[1, e])
-                cp[e] = add(cp[e], cb[e])
-
-            c_copy(e, 1).start()
-
-    c_dot(3)
-    c_dot(0)
-    c_step(0)
-
+    c_dot(odd)
+    c_dot(odd + 2)
     for copy in raw_q:
         copy.wait_recv()
     qf[0] = add(qf[0], qp[1, 0:half])
@@ -407,11 +387,7 @@
     for copy in sum_q:
         copy.start()
 
-    c_dot(2)
-    c_dot(1)
-    c_step(1)
-
-    kw = mm(xt[...], gd[:, pl.ds(pl.multiple_of((5 * me.x + 4) * UNIT, UNIT), UNIT)])
+    kw = w_dot(me.x, 4, 1)
     for copy in own_k + sum_k:
         copy.wait_recv()
     kv[me.z] = (kw + kl[...].astype(F32) + kr[...].astype(F32)).astype(BF16)
@@ -428,8 +404,12 @@
     def _():
         kv_send(me.z, 1).start()
 
-    c_step(2)
-    qw = mm(xt[...], gd[:, pl.ds(pl.multiple_of(5 * me.x * UNIT, UNIT), 4 * UNIT)])
+    for copy in c_near:
+        copy.wait_recv()
+    cb[0] = add(cp[away], ca[away // 2])
+    c_far = remote(cb.at[0], cb.at[1], cs.at[2], crv.at[2], me.at(z=away))
+    c_far.start()
+    qw = w_dot(me.x, 0, 4)
 
     for step in range(1, 4):
         low = me.z - step
@@ -463,17 +443,10 @@
     square = (qw + ql[...].astype(F32) + qr[...].astype(F32)).astype(BF16)
     out_q[...] = update_of(left_of(square), square)
 
-    for d in range(4):
-        @pl.when(me.z == d)
-        def _():
-            total = cp[d].astype(F32)
-            if d > 0:
-                wait_for(ca.at[d], crv.at[0, d])
-                total += ca[d].astype(F32)
-            if d < 3:
-                wait_for(cb.at[d], crv.at[1, d])
-                total += cb[d].astype(F32)
-            out_c[...] = total.astype(BF16)
+    c_far.wait_recv()
+    out_c[...] = (
+        cp[me.z].astype(F32) + ca[me.z // 2].astype(F32) + cb[1].astype(F32)
+    ).astype(BF16)
 
     for k in range(5):
         q, slot = slot_of(5 * me.owner + k)
@@ -511,11 +484,7 @@
             wait_for(block, xs.at[1, origin])
             wait_for(kv.at[origin], ss.at[1, origin])
 
-        @pl.when(me.z != origin)
-        def _():
-            wait_for(cp.at[origin], cs.at[origin])
-
-    for copy in raw_k + own_k + sum_k + raw_q + own_q + sum_q:
+    for copy in raw_k + own_k + sum_k + raw_q + own_q + sum_q + c_near + [c_far]:
         copy.wait_send()
 
 
@@ -581,8 +550,8 @@
             space(rows, BLOCK),
             space(4, rows, UNIT),
             space(4, tokens, rows),
-            space(4, tokens, rows),
-            space(4, tokens, rows),
+            space(2, tokens, rows),
+            space(2, tokens, rows),
             dma(5, 2),
             dma(SLOTS, 3),
             dma(SLOTS, 4),
@@ -601,8 +570,8 @@
             dma(4),
             dma(2, 4),
             dma(4),
-            dma(4),
-            dma(2, 4),
+            dma(3),
+            dma(3),
         ],
         compiler_params=pltpu.CompilerParams(
             collective_id=0, has_side_effects=True, vmem_limit_bytes=VMEM_LIMIT

time: 129 us -> 119 us (0.922)
  Pallas kernels: 125 us -> 115 us
    pallas_call x1, Pallas kernels: 125 us -> 115 us  [body(): pl.pallas_call(fused_kernel, name='fused', out_shape=(shape((tokens, rows...]
where the time goes in v3:
time: 119 us
  Pallas kernels  115 us (97%)
  local copies, waits for them, and re-layouts  3.41 us (3%)
    pallas_call x1, Pallas kernels, body(): pl.pallas_call(fused_kernel, name='fused', out_shape=(shape((tokens, rows...  115 us
    unnamed x7, local copies, waits for them, and re-layouts  3.41 us

profile of v3, /device:TPU:10, one launch (start us, length us, event | category | flops | bytes accessed | tf_op | source)
XLA Modules:
  0.0 118.8 jit_solution(3061213563622377954)
XLA Ops:
  0.6 114.7 %fused.1 = (bf16[256,512]{1,0:T(8,128)(2,1)}, bf16[512,512]{1,0:T(8,128)(2,1)}, bf16[512,128]{1,0:T(8,128)(2,1)}) custom-call(bf16[256,512]{1,0:T(8,128)(2,1)} %x_ref.1, bf16[256,640]{1,0:T(8,128)(2,1)} %g_ref.1, bf16[512,640]{1,0:T(8,128)(2,1)} %p_ref.1), custom_call_target="tpu_custom_call" | custom-call | tf_op jit(solution)/shard_map/fused/pallas_call | solution.py:528
  115.4 0.0 copy-start
  115.4 1.7 %copy.9 = bf16[256,512]{1,0:T(8,128)(2,1)} copy(bf16[256,512]{1,0:T(8,128)(2,1)} %get-tuple-element.6) | data formatting | bytes 524288
  117.1 0.0 copy-done
  117.1 0.0 copy-start.1
  117.1 0.8 copy.10
  117.9 0.2 copy-done.1
  118.1 0.7 copy.11
Async XLA Ops:
  115.4 1.7 %copy-start = (bf16[512,512]{1,0:T(8,128)(2,1)S(1)}, bf16[512,512]{1,0:T(8,128)(2,1)}, u32[]{:S(2)}) copy-start(bf16[512,512]{1,0:T(8,128)(2,1)} %get-tuple-element.7) | copy-start | bytes 1572868
  117.1 1.0 copy-start.1

commit v4 on v3

--- a/solution.py
+++ b/solution.py
@@ -76,9 +76,9 @@
 
 
 def fused_kernel(
-    x_ref, g_ref, p_ref, out_c, out_q, out_kv,
+    x_ref, g_ref, p_ref, out_c, out_q, out_kv, pin,
     xg, xt, gd, pg, kp, qp, kf, qf, kl, kr, ql, qr, kv, cp, ca, cb,
-    gs1, gs, gr, ps1, ps, pr, xs, xr,
+    gs1, gs, gr, p0s, p0r, p1s, p1r, ps, pf, pr, pl_sem, xs, xr,
     fks, fkr, fqs, fqr, ks, kvr, qs, qvr, ss, sr, cs, crv,
 ):
     me = Place()
@@ -91,7 +91,7 @@
     for step in range(1, 8):
         far = (me.zh * 4 + me.z + step) % 8
         devices.append(me.at(z=far % 4, zh=far // 4))
-    devices += [me.at(y=yp), me.at(y=ym), me.at(c=1 - me.c), me.at(x=xp), me.at(x=xm)]
+    devices += [me.at(y=yp), me.at(y=ym), me.at(c=1 - me.c), me.at(x=xp), me.at(x=xm), me.at(x=xo)]
     greet(devices)
 
     def mine(z):
@@ -99,6 +99,23 @@
 
     def wait_for(part, sem):
         pltpu.make_async_copy(part, part, sem).wait()
+
+    quarter = rows // 4
+    width = p_ref.shape[1]
+
+    def share(x):
+        return pl.ds(pl.multiple_of(x * quarter, quarter), quarter)
+
+    def group_cols(group):
+        return pl.ds(pl.multiple_of(group * width, UNIT), width)
+
+    scatter = []
+    for step, x in ((1, xp), (3, xm), (2, xo)):
+        copy = remote(
+            p_ref.at[share(x)], pin.at[me.x], p0s.at[step], p0r.at[me.x], me.at(x=x)
+        )
+        copy.start()
+        scatter.append(copy)
 
     for k in range(5):
         q, slot = slot_of(5 * me.owner + k)
@@ -115,22 +132,33 @@
             def _():
                 remote(src, dst, gs1.at[k, zh], gr.at[slot, me.z], me.at(z=q, zh=zh)).start()
 
-    for k in range(5):
-        q, slot = slot_of(5 * me.dp + k)
-        src = p_ref.at[:, k * UNIT : (k + 1) * UNIT]
-        dst = pg.at[:, cols(slot)]
-
-        @pl.when(q == me.z)
-        def _():
-            pltpu.make_async_copy(src, dst, pr.at[slot, 0]).start()
-
-        @pl.when(q != me.z)
-        def _():
-            remote(src, dst, ps1.at[k], pr.at[slot, 0], me.at(z=q)).start()
-
     def x_send(src, origin, side):
         to = me.z + 1 if side == 0 else me.z - 1
         return remote(src, xg.at[mine(origin)], xs.at[side, origin], xr.at[origin], me.at(z=to))
+
+    def quarter_unit(x, step, k):
+        unit = 5 * (4 * x + me.z) + k
+        q, slot = slot_of(unit)
+        kv_unit = unit >> 6
+        group = (unit >> 4) + kv_unit * ((unit >> 2) - 16 - (unit >> 4))
+        at = slice(k * UNIT, (k + 1) * UNIT)
+        src = p_ref.at[share(me.x), at] if step == 0 else pin.at[x, :, at]
+        return q, src, pg.at[share(me.x), cols(slot)], group
+
+    quarters = ((0, me.x), (1, xm), (3, xp), (2, xo))
+    for step, x in quarters:
+        if step:
+            wait_for(pin.at[x], p0r.at[x])
+        for k in range(5):
+            q, src, dst, group = quarter_unit(x, step, k)
+
+            @pl.when(q == me.z)
+            def _():
+                pltpu.make_async_copy(src, dst, p1r.at[group]).start()
+
+            @pl.when(q != me.z)
+            def _():
+                remote(src, dst, p1s.at[step, k], p1r.at[group], me.at(z=q)).start()
 
     own_x = pltpu.make_async_copy(x_ref, xg.at[mine(me.z)], xr.at[me.z])
     own_x.start()
@@ -180,16 +208,13 @@
         device = (me.at(y=yp), me.at(y=ym), me.at(c=1 - me.c))[way]
         return remote(part, part, gs.at[slot, way], gr.at[slot, index], device)
 
-    def p_unit(x, z, k):
-        q, slot = slot_of(5 * (4 * x + z) + k)
-        whole = pg.at[:, cols(slot)]
-        upper = pg.at[0:half, cols(slot)]
-        lower = pg.at[half:rows, cols(slot)]
-        return q == me.z, slot, whole, upper, lower
-
-    def p_send(part, slot, way, index=0):
-        device = (me.at(x=xp), me.at(x=xm))[way]
-        return remote(part, part, ps.at[slot, way], pr.at[slot, index], device)
+    def p_block(x, group):
+        start = x * quarter
+        middle = quarter // 2
+        whole = pg.at[share(x), group_cols(group)]
+        upper = pg.at[pl.ds(pl.multiple_of(start, middle), middle), group_cols(group)]
+        lower = pg.at[pl.ds(pl.multiple_of(start + middle, middle), middle), group_cols(group)]
+        return whole, upper, lower
 
     def g_origin(k, waiting):
         for zh in range(2):
@@ -244,42 +269,30 @@
                 def _():
                     wait_for(whole, gr.at[slot, 0])
 
-    def p_origin(k, waiting):
-        for z in range(4):
-            ok, slot, whole, upper, lower = p_unit(me.x, z, k)
-
-            @pl.when(ok)
-            def _():
-                if waiting:
-                    for way in range(2):
-                        wait_for(whole, ps.at[slot, way])
-                else:
-                    wait_for(whole, pr.at[slot, 0])
-                    for way in range(2):
-                        p_send(whole, slot, way).start()
-
-    def p_next(k, waiting):
-        for z in range(4):
-            for side, x in ((0, xm), (1, xp)):
-                ok, slot, whole, upper, lower = p_unit(x, z, k)
-                part = upper if side == 0 else lower
-
-                @pl.when(ok)
-                def _():
-                    if waiting:
-                        wait_for(part, ps.at[slot, side])
-                    else:
-                        wait_for(whole, pr.at[slot, 0])
-                        p_send(part, slot, side, side).start()
-
-    def p_last(k):
-        for z in range(4):
-            ok, slot, whole, upper, lower = p_unit(xo, z, k)
-
-            @pl.when(ok)
-            def _():
-                wait_for(upper, pr.at[slot, 0])
-                wait_for(lower, pr.at[slot, 1])
+    def p_origin(group):
+        whole, upper, lower = p_block(me.x, group)
+        wait_for(whole, p1r.at[group])
+        for way, x in ((0, xp), (1, xm)):
+            remote(whole, whole, ps.at[way, group], pr.at[me.x, group], me.at(x=x)).start()
+
+    def p_next(group):
+        whole, upper, lower = p_block(xm, group)
+        wait_for(whole, pr.at[xm, group])
+        remote(upper, upper, pf.at[0, group], pr.at[xm, group], me.at(x=xp)).start()
+        whole, upper, lower = p_block(xp, group)
+        wait_for(whole, pr.at[xp, group])
+        remote(lower, lower, pf.at[1, group], pl_sem.at[group], me.at(x=xm)).start()
+
+    def p_last(group):
+        whole, upper, lower = p_block(xo, group)
+        wait_for(upper, pr.at[xo, group])
+        wait_for(lower, pl_sem.at[group])
+
+    def p_sent(group):
+        for way in range(2):
+            wait_for(p_block(me.x, group)[0], ps.at[way, group])
+        wait_for(p_block(xm, group)[1], pf.at[0, group])
+        wait_for(p_block(xp, group)[2], pf.at[1, group])
 
     @pl.loop(0, 5)
     def _(k):
@@ -287,15 +300,23 @@
 
     @pl.loop(0, 5)
     def _(k):
-        p_origin(k, False)
         g_next(k, False)
+
+        @pl.when(k < 4)
+        def _():
+            p_origin(k)
+
 
     x_step(1)
 
     @pl.loop(0, 5)
     def _(k):
-        p_next(k, False)
         g_last(k, False)
+
+        @pl.when(k < 4)
+        def _():
+            p_next(k)
+
 
     x_step(2)
 
@@ -309,9 +330,9 @@
     def _(k):
         g_sibling(k)
 
-    @pl.loop(0, 5)
-    def _(k):
-        p_last(k)
+    @pl.loop(0, 4)
+    def _(group):
+        p_last(group)
 
     def w_dot(x, first, count):
         at = pl.ds(pl.multiple_of((5 * x + first) * UNIT, UNIT), count * UNIT)
@@ -456,20 +477,23 @@
             def _():
                 wait_for(src, gs1.at[k, zh])
 
-        q, slot = slot_of(5 * me.dp + k)
-        psrc = p_ref.at[:, k * UNIT : (k + 1) * UNIT]
-
-        @pl.when(q != me.z)
-        def _():
-            wait_for(psrc, ps1.at[k])
+    for step, x in quarters:
+        for k in range(5):
+            q, src, dst, group = quarter_unit(x, step, k)
+
+            @pl.when(q != me.z)
+            def _():
+                wait_for(src, p1s.at[step, k])
+
+    @pl.loop(0, 4)
+    def _(group):
+        p_sent(group)
 
     @pl.loop(0, 5)
     def _(k):
         g_origin(k, True)
         g_next(k, True)
         g_last(k, True)
-        p_origin(k, True)
-        p_next(k, True)
 
     for origin in range(4):
         block = xg.at[origin * tokens : (origin + 1) * tokens]
@@ -484,7 +508,7 @@
             wait_for(block, xs.at[1, origin])
             wait_for(kv.at[origin], ss.at[1, origin])
 
-    for copy in raw_k + own_k + sum_k + raw_q + own_q + sum_q + c_near + [c_far]:
+    for copy in raw_k + own_k + sum_k + raw_q + own_q + sum_q + c_near + [c_far] + scatter:
         copy.wait_send()
 
 
@@ -532,9 +556,10 @@
             shape((tokens, rows), BF16),
             shape((rows, BLOCK), BF16),
             shape((rows, UNIT), BF16),
+            shape((4, rows // 4, projection.shape[1]), BF16),
         ),
         in_specs=[pl.BlockSpec(memory_space=pl.ANY)] * 3,
-        out_specs=(vmem, vmem, vmem),
+        out_specs=(vmem, vmem, vmem, pl.BlockSpec(memory_space=pl.ANY)),
         scratch_shapes=[
             space(4 * tokens, rows),
             space(rows, 4 * tokens),
@@ -555,9 +580,14 @@
             dma(5, 2),
             dma(SLOTS, 3),
             dma(SLOTS, 4),
-            dma(5),
-            dma(SLOTS, 2),
-            dma(SLOTS, 2),
+            dma(4),
+            dma(4),
+            dma(4, 5),
+            dma(4),
+            dma(2, 4),
+            dma(2, 4),
+            dma(4, 4),
+            dma(4),
             dma(2, 4),
             dma(4),
             dma(2),
@@ -576,7 +606,7 @@
         compiler_params=pltpu.CompilerParams(
             collective_id=0, has_side_effects=True, vmem_limit_bytes=VMEM_LIMIT
         ),
-    )(layer_input, output_grads, projection)
+    )(layer_input, output_grads, projection)[:3]
 
 
 def solution(mesh):

time: 119 us -> 114 us (0.958); the launches traced: 119 us -> 112 us
  Pallas kernels: 115 us -> 108 us
    pallas_call x1, Pallas kernels: 115 us -> 108 us  [body(): pl.pallas_call(fused_kernel, name='fused', out_shape=(shape((tokens, rows...]
where the time goes in v4:
time: 114 us; the launch traced here: 112 us
  Pallas kernels  108 us (95%)
  local copies, waits for them, and re-layouts  3.41 us (3%)
    pallas_call x1, Pallas kernels, body(): pl.pallas_call(fused_kernel, name='fused', out_shape=(shape((tokens, rows...  108 us
    unnamed x7, local copies, waits for them, and re-layouts  3.41 us

profile of v4, /device:TPU:10, one launch (start us, length us, event | category | flops | bytes accessed | tf_op | source)
XLA Modules:
  0.0 112.3 jit_solution(15448776703590502053)
XLA Ops:
  0.6 108.2 %fused.1 = (bf16[256,512]{1,0:T(8,128)(2,1)}, bf16[512,512]{1,0:T(8,128)(2,1)}, bf16[512,128]{1,0:T(8,128)(2,1)}, bf16[4,128,640]{2,1,0:T(8,128)(2,1)}) custom-call(bf16[256,512]{1,0:T(8,128)(2,1)} %x_ref.1, bf16[256,640]{1,0:T(8,128)(2,1)} %g_ref.1, bf16[512,640]{1,0:T(8,128)(2,1)} %p_ref.1), custom_call_target="tpu_custom_call" | custom-call | tf_op jit(solution)/shard_map/fused/pallas_call | solution.py:552
  108.9 0.0 copy-start
  108.9 1.7 %copy.9 = bf16[256,512]{1,0:T(8,128)(2,1)} copy(bf16[256,512]{1,0:T(8,128)(2,1)} %get-tuple-element.12) | data formatting | bytes 524288
  110.6 0.0 copy-done
  110.6 0.0 copy-start.1
  110.6 0.8 copy.10
  111.4 0.2 copy-done.1
  111.6 0.7 copy.11
Async XLA Ops:
  108.9 1.7 %copy-start = (bf16[512,512]{1,0:T(8,128)(2,1)S(1)}, bf16[512,512]{1,0:T(8,128)(2,1)}, u32[]{:S(2)}) copy-start(bf16[512,512]{1,0:T(8,128)(2,1)} %get-tuple-element.13) | copy-start | bytes 1572868
  110.6 1.0 copy-start.1

commit v5 on v4

--- a/solution.py
+++ b/solution.py
@@ -76,7 +76,7 @@
 
 
 def fused_kernel(
-    x_ref, g_ref, p_ref, out_c, out_q, out_kv, pin,
+    x_ref, g_ref, p_ref, out_kv, out_c, out_q, pin,
     xg, xt, gd, pg, kp, qp, kf, qf, kl, kr, ql, qr, kv, cp, ca, cb,
     gs1, gs, gr, p0s, p0r, p1s, p1r, ps, pf, pr, pl_sem, xs, xr,
     fks, fkr, fqs, fqr, ks, kvr, qs, qvr, ss, sr, cs, crv,
@@ -228,8 +228,11 @@
                 else:
                     for t in range(4):
                         wait_for(gd.at[t * tokens : (t + 1) * tokens, cols(slot)], gr.at[slot, t])
-                    for way in range(3):
-                        g_send(whole, slot, way).start()
+                    g_send(upper, slot, 0, 0).start()
+                    g_send(lower, slot, 1, 1).start()
+                    g_send(lower, slot, 0, 1).start()
+                    g_send(upper, slot, 1, 0).start()
+                    g_send(whole, slot, 2).start()
 
     def g_next(k, waiting):
         for zh in range(2):
@@ -243,8 +246,10 @@
                         wait_for(part, gs.at[slot, side])
                         wait_for(whole, gs.at[slot, 2])
                     else:
-                        wait_for(whole, gr.at[slot, 0])
+                        rest = lower if side == 0 else upper
+                        wait_for(part, gr.at[slot, side])
                         g_send(part, slot, side, side).start()
+                        wait_for(rest, gr.at[slot, 1 - side])
                         g_send(whole, slot, 2).start()
 
     def g_last(k, waiting):
@@ -459,16 +464,6 @@
         gram += left_of(kv[part])
     out_kv[...] = update_of(gram, kv[me.z])
 
-    for copy in own_q + sum_q:
-        copy.wait_recv()
-    square = (qw + ql[...].astype(F32) + qr[...].astype(F32)).astype(BF16)
-    out_q[...] = update_of(left_of(square), square)
-
-    c_far.wait_recv()
-    out_c[...] = (
-        cp[me.z].astype(F32) + ca[me.z // 2].astype(F32) + cb[1].astype(F32)
-    ).astype(BF16)
-
     for k in range(5):
         q, slot = slot_of(5 * me.owner + k)
         src = g_ref.at[:, k * UNIT : (k + 1) * UNIT]
@@ -494,6 +489,16 @@
         g_origin(k, True)
         g_next(k, True)
         g_last(k, True)
+
+    for copy in own_q + sum_q:
+        copy.wait_recv()
+    square = (qw + ql[...].astype(F32) + qr[...].astype(F32)).astype(BF16)
+    out_q[...] = update_of(left_of(square), square)
+
+    c_far.wait_recv()
+    out_c[...] = (
+        cp[me.z].astype(F32) + ca[me.z // 2].astype(F32) + cb[1].astype(F32)
+    ).astype(BF16)
 
     for origin in range(4):
         block = xg.at[origin * tokens : (origin + 1) * tokens]
@@ -549,13 +554,13 @@
     def space(*dims):
         return pltpu.VMEM(dims, BF16)
 
-    return pl.pallas_call(
+    update_kv, grad_input, update_query, _ = pl.pallas_call(
         fused_kernel,
         name="fused",
         out_shape=(
+            shape((rows, UNIT), BF16),
             shape((tokens, rows), BF16),
             shape((rows, BLOCK), BF16),
-            shape((rows, UNIT), BF16),
             shape((4, rows // 4, projection.shape[1]), BF16),
         ),
         in_specs=[pl.BlockSpec(memory_space=pl.ANY)] * 3,
@@ -606,7 +611,8 @@
         compiler_params=pltpu.CompilerParams(
             collective_id=0, has_side_effects=True, vmem_limit_bytes=VMEM_LIMIT
         ),
-    )(layer_input, output_grads, projection)[:3]
+    )(layer_input, output_grads, projection)
+    return (grad_input, update_query, update_kv)
 
 
 def solution(mesh):

time: 114 us -> 114 us (level)
  no operation moved by 1% of the time
where the time goes in v5:
time: 114 us; the launch traced here: 112 us
  Pallas kernels  108 us (95%)
  local copies, waits for them, and re-layouts  3.41 us (3%)
    pallas_call x1, Pallas kernels, body(): pl.pallas_call(fused_kernel, name='fused', out_shape=(shape((rows, UNIT),...  108 us
    unnamed x7, local copies, waits for them, and re-layouts  3.41 us

profile of v5, /device:TPU:10, one launch (start us, length us, event | category | flops | bytes accessed | tf_op | source)
XLA Modules:
  0.0 112.3 jit_solution(6097273111135193716)
XLA Ops:
  0.6 108.2 %fused.1 = (bf16[512,128]{1,0:T(8,128)(2,1)}, bf16[256,512]{1,0:T(8,128)(2,1)}, bf16[512,512]{1,0:T(8,128)(2,1)}, bf16[4,128,640]{2,1,0:T(8,128)(2,1)}) custom-call(bf16[256,512]{1,0:T(8,128)(2,1)} %x_ref.1, bf16[256,640]{1,0:T(8,128)(2,1)} %g_ref.1, bf16[512,640]{1,0:T(8,128)(2,1)} %p_ref.1), custom_call_target="tpu_custom_call" | custom-call | tf_op jit(solution)/shard_map/fused/pallas_call | solution.py:557
  108.9 0.0 copy-start
  108.9 1.7 %copy.9 = bf16[256,512]{1,0:T(8,128)(2,1)} copy(bf16[256,512]{1,0:T(8,128)(2,1)} %get-tuple-element.12) | data formatting | bytes 524288
  110.6 0.0 copy-done
  110.6 0.0 copy-start.1
  110.6 0.8 copy.10
  111.4 0.2 copy-done.1
  111.6 0.7 copy.11
Async XLA Ops:
  108.9 1.7 %copy-start = (bf16[512,512]{1,0:T(8,128)(2,1)S(1)}, bf16[512,512]{1,0:T(8,128)(2,1)}, u32[]{:S(2)}) copy-start(bf16[512,512]{1,0:T(8,128)(2,1)} %get-tuple-element.13) | copy-start | bytes 1572868
  110.6 1.0 copy-start.1
